TPU v7x, 32 devices: a whole 2x2x4 slice. The times are simulated.
32 devices in a mesh: dp: 8 (over y, x, core), mp: 4 (over z).
Axes of the slice: x: 2, y: 2, z: 4, core: 2. Of those that a mesh axis runs over, the one named last changes fastest.
Arguments:
- tokens: bfloat16 [4096, 1024], P('dp', 'mp'), may hold values from -150 to 150
- pre_gain: bfloat16 [1024], P('mp'), may hold values from 0.25 to 1.75
- input_weight: bfloat16 [3, 1024, 1024], P(None, 'dp', 'mp'), may hold values from -0.125 to 0.125
- output_weight: bfloat16 [1024, 1024], P('mp', 'dp'), may hold values from -1 to 1
- position_bias: bfloat16 [16, 512, 512], P('mp'), may hold values from -3 to 353
- post_gain: bfloat16 [1024], P('mp'), may hold values from 0.25 to 1.75
Outputs:
- stream: bfloat16 [4096, 1024], P('dp', 'mp')
- normed: bfloat16 [4096, 1024], P('dp', 'mp')
All inputs are finite; a program needn't handle non-finite values.
Results may differ from a plain program's by a relative error of at most 0.013.
Values may be sent and summed in bfloat16 or wider, within the bound.
A program may use at most 64 MiB of HBM per device.

v0:
```python
import jax
import jax.numpy as jnp
from jax import lax
from jax.sharding import PartitionSpec as P

epsilon = 1e-06


def attend_all(mixed_heads, position_bias):
    row_count = mixed_heads.shape[1]
    inner_width = mixed_heads.shape[2]
    head_count = position_bias.shape[0]
    seq_len = position_bias.shape[1]
    grouped = mixed_heads.reshape(
        3, row_count // seq_len, seq_len, head_count, inner_width // head_count
    )
    bias_wide = position_bias.astype(jnp.float32)

    def one_sequence(sequence):
        sequence_block = lax.dynamic_index_in_dim(grouped, sequence, 1, keepdims=False)
        scores = (
            jnp.einsum(
                "qhd,khd->hqk",
                sequence_block[0],
                sequence_block[1],
                preferred_element_type=jnp.float32,
            )
            + bias_wide
        )
        row_max = jnp.max(scores, axis=2, keepdims=True)
        weights = jnp.exp(scores - row_max)
        probabilities = (weights / jnp.sum(weights, axis=2, keepdims=True)).astype(jnp.bfloat16)
        context = jnp.einsum(
            "hqk,khd->qhd", probabilities, sequence_block[2], preferred_element_type=jnp.float32
        )
        return context.reshape(seq_len, inner_width).astype(jnp.bfloat16)

    stacked = lax.map(one_sequence, jnp.arange(row_count // seq_len, dtype=jnp.int32))
    return stacked.reshape(row_count, inner_width)


def on_device(tokens, pre_gain, input_weight, output_weight, position_bias, post_gain):
    rows_all, gain_all = (
        lax.all_gather(tokens, "mp", axis=1, tiled=True),
        lax.all_gather(pre_gain, "mp", axis=0, tiled=True),
    )
    widened = rows_all.astype(jnp.float32)
    inverse_rms = lax.rsqrt(jnp.mean(widened * widened, axis=1, keepdims=True) + epsilon)
    normed_in = (widened * inverse_rms * gain_all.astype(jnp.float32)).astype(jnp.bfloat16)
    feature_count = tokens.shape[1]
    projected = jnp.einsum(
        "td,kdi->kti",
        normed_in,
        lax.all_gather(input_weight, "dp", axis=1, tiled=True),
        preferred_element_type=jnp.float32,
    )
    context = attend_all(projected.astype(jnp.bfloat16), position_bias)
    partial_value = jnp.dot(
        context,
        lax.all_gather(output_weight, "dp", axis=1, tiled=True),
        preferred_element_type=jnp.float32,
    )
    attention_out = lax.psum_scatter(
        partial_value.astype(jnp.bfloat16), "mp", scatter_dimension=1, tiled=True
    ).astype(jnp.float32)
    stream = (tokens.astype(jnp.float32) + attention_out).astype(jnp.bfloat16)
    restored = lax.optimization_barrier(stream).astype(jnp.float32)
    squares = lax.psum(jnp.sum(restored * restored, axis=1), "mp")
    post_rms = lax.rsqrt(squares[:, None] / (feature_count * lax.axis_size("mp")) + epsilon)
    normed = (restored * post_rms * post_gain.astype(jnp.float32)).astype(jnp.bfloat16)
    return (stream, normed)


def solution(mesh):
    return jax.shard_map(
        on_device,
        mesh=mesh,
        in_specs=(
            P("dp", "mp"),
            P("mp"),
            P(None, "dp", "mp"),
            P("mp", "dp"),
            P("mp", None, None),
            P("mp"),
        ),
        out_specs=(P("dp", "mp"), P("dp", "mp")),
        check_vma=False,
    )
```

profile of v0, /device:TPU:0, one launch (start us, length us, event | category | flops | bytes accessed | tf_op | source)
XLA Modules:
  0.0 123.4 jit_solution(2190378064825369234)
XLA Ops:
  7.2 0.0 all-gather.4.cloned.1.call-start
  7.2 0.7 all-gather.4.cloned.1.call-update
  7.9 0.0 all-gather.6.cloned.1.call-start
  7.9 1.7 %copy.11 = bf16[3,128,256]{1,2,0:T(8,128)(2,1)} copy(bf16[3,128,256]{2,1,0:T(8,128)(2,1)} %param.8) | data formatting | bytes 393216 | tf_op args[2]
  9.7 0.0 all-gather.6.cloned.1.call-update
  9.7 0.0 reduce-scatter.2.cloned.1.call-start
  9.8 0.7 reshape.34
  10.4 12.6 %all-gather = bf16[4,1,256]{2,1,0:T(2,128)(2,1)S(1)} all-gather(bf16[1,1,256]{2,1,0:T(2,128)(2,1)S(1)} %reshape.34), channel_id=1, replica_groups=mesh['dp'=8,'mp'=4] {'mp'}, dimensions={0}, use_global_device_ids=true | all-gather | bytes 2560 | tf_op jit(solution)/shard_map/all_gather | solution.py:45
  23.1 0.0 copy-start.2
  23.1 2.8 %copy.12 = bf16[4,512,512]{1,2,0:T(8,128)(2,1)S(1)} copy(bf16[4,512,512]{2,1,0:T(8,128)(2,1)} %param.10) | data formatting | bytes 4194304 | tf_op args[4]
  25.9 0.0 copy-done.2
  25.9 10.0 %all_gather.15 = bf16[256,1024]{1,0:T(8,128)(2,1)S(1)} all-gather(bf16[256,128]{1,0:T(8,128)(2,1)S(1)} %copy-done.2), channel_id=1, replica_groups=mesh['dp'=8,'mp'=4] {'dp'}, dimensions={1}, use_global_device_ids=true | all-gather | bytes 589824 | tf_op jit(solution)/shard_map/all_gather | solution.py:60
  35.9 6.2 %all-gather.4.cloned.1.call-done = bf16[512,1024]{1,0:T(8,128)(2,1)} async-done(((bf16[512,256]{1,0:T(8,128)(2,1)}), bf16[512,1024]{1,0:T(8,128)(2,1)}) %all-gather.4.cloned.1.call-update) | async-done | bytes 1048592 | tf_op jit(solution)/shard_map/all_gather | solution.py:44
  42.1 1.5 %fusion.2 = f32[512]{0:T(512)S(1)} fusion(bf16[512,1024]{1,0:T(8,128)(2,1)} %all-gather.4.cloned.1.call-done), kind=kLoop, calls=%fused_computation.7 | loop fusion | flops 1572352 | bytes 1050624 | tf_op jit(solution)/shard_map/reduce_sum | solution.py:48
  43.6 25.1 %all-gather.6.cloned.1.call-done = bf16[3,1024,256]{1,2,0:T(8,128)(2,1)} async-done(((bf16[3,128,256]{1,2,0:T(8,128)(2,1)}), bf16[3,1024,256]{1,2,0:T(8,128)(2,1)}) %all-gather.6.cloned.1.call-update) | async-done | bytes 1572880 | tf_op jit(solution)/shard_map/all_gather | solution.py:54
  68.7 2.8 %fusion.6 = bf16[3,512,256]{1,2,0:T(8,128)(2,1)S(1)} fusion(bf16[3,1024,256]{1,2,0:T(8,128)(2,1)} %all-gather.6.cloned.1.call-done, bf16[512,1024]{1,0:T(8,128)(2,1)} %all-gather.4.cloned.1.call-done, f32[1024]{0:T(1024)S(1)} %bitcast.26, f32[512]{0:T(512)S(1)} %add_rsqrt_fusion.1), kind=kOutput, calls=%fused_computation.13 | convolution fusion | flops 807796736 | bytes 3414016 | tf_op jit(solution)/shard_map/td,kdi->kti/dot_general | solution.py:51
  71.5 0.8 fusion.18
  72.3 1.5 %fusion.19 = f32[4,512]{1,0:T(4,128)S(1)} fusion(bf16[4,512,512]{1,2,0:T(8,128)(2,1)S(1)} %copy.12, bf16[512,4,64]{0,2,1:T(8,128)(2,1)S(1)} %bitcast.23, bf16[512,4,64]{0,2,1:T(8,128)(2,1)S(1)} %bitcast.21), kind=kOutput, calls=%fused_computation.29 | convolution fusion | flops 138412544 | bytes 2629632 | tf_op jit(solution)/shard_map/while/body/eval_jaxpr/sub | solution.py:31
  73.8 2.9 %fusion.7 = bf16[4,64,512]{2,1,0:T(8,128)(2,1)S(1)} fusion(bf16[512,4,64]{0,2,1:T(8,128)(2,1)} %bitcast.25, f32[4,512]{1,0:T(4,128)S(1)} %fusion.19, bf16[4,512,512]{1,2,0:T(8,128)(2,1)S(1)} %copy.12, bf16[512,4,64]{0,2,1:T(8,128)(2,1)S(1)} %bitcast.24, bf16[512,4,64]{0,2,1:T(8,128)(2,1)S(1)} %bitcast.22), kind=kOutput, calls=%fused_computation.14 | convolution fusion | flops 273811968 | bytes 3153920 | tf_op jit(solution)/shard_map/while/body/eval_jaxpr/hqk,khd->qhd/dot_general | solution.py:33
  76.6 0.0 copy-start.3
  76.6 0.0 copy-start.1
  76.6 1.4 %convolution_convert_fusion = bf16[512,1024]{1,0:T(8,128)(2,1)} fusion(bf16[512,256]{0,1:T(8,128)(2,1)S(1)} %bitcast.20, bf16[256,1024]{1,0:T(8,128)(2,1)S(1)} %all_gather.15), kind=kOutput, calls=%fused_computation.11 | convolution fusion | flops 268959744 | bytes 1835008 | tf_op jit(solution)/shard_map/dot_general | solution.py:58
  78.1 0.0 reduce-scatter.2.cloned.1.call-update
  78.1 0.0 copy-done.3
  78.1 27.4 %reduce-scatter.2.cloned.1.call-done = bf16[512,256]{1,0:T(8,128)(2,1)} async-done(((bf16[512,1024]{1,0:T(8,128)(2,1)}), bf16[512,256]{1,0:T(8,128)(2,1)}) %reduce-scatter.2.cloned.1.call-update) | async-done | bytes 262160 | tf_op jit(solution)/shard_map/reduce_scatter | solution.py:63
  105.6 0.0 copy-done.1
  105.6 1.0 add_convert_fusion
  106.6 0.0 copy-start
  106.6 0.1 fusion.12
  106.7 9.3 %psum.7 = f32[512]{0:T(512)S(1)} all-reduce(f32[512]{0:T(512)S(1)} %fusion.12), channel_id=1, replica_groups=mesh['dp'=8,'mp'=4] {'mp'}, use_global_device_ids=true, to_apply=%region_5.6 | all-reduce | flops 512 | bytes 4096 | tf_op jit(solution)/shard_map/psum | solution.py:68
  116.0 0.8 fusion.14
  116.9 0.0 copy-done
  (4 shorter events, 0.0 us)
Async XLA Ops:
  7.2 35.0 %all-gather.4.cloned.1.call-start = ((), (), s32[]{:S(2)}) async-start(), calls=%async_computation.1 | async-start | bytes 1310720 | tf_op jit(solution)/shard_map/all_gather | solution.py:44
  7.9 60.8 %all-gather.6.cloned.1.call-start = ((), (), s32[]{:S(2)}) async-start(), calls=%async_computation.2 | async-start | bytes 1769472 | tf_op jit(solution)/shard_map/all_gather | solution.py:54
  9.7 95.8 %reduce-scatter.2.cloned.1.call-start = ((), (), s32[]{:S(2)}) async-start(), calls=%async_computation.3 | async-start | bytes 1310720 | tf_op jit(solution)/shard_map/reduce_scatter | solution.py:63
  23.1 2.8 %copy-start.2 = (bf16[256,128]{1,0:T(8,128)(2,1)S(1)}, bf16[256,128]{1,0:T(8,128)(2,1)}, u32[]{:S(2)}) copy-start(bf16[256,128]{1,0:T(8,128)(2,1)} %param.9) | copy-start | bytes 196612
  76.6 1.5 %copy-start.3 = (bf16[256]{0:T(256)(128)(2,1)S(1)}, bf16[256]{0:T(256)(128)(2,1)}, u32[]{:S(2)}) copy-start(bf16[256]{0:T(256)(128)(2,1)} %param.11) | copy-start | bytes 1540
  76.6 28.9 %copy-start.1 = (bf16[512,256]{1,0:T(8,128)(2,1)S(1)}, bf16[512,256]{1,0:T(8,128)(2,1)}, u32[]{:S(2)}) copy-start(bf16[512,256]{1,0:T(8,128)(2,1)} %param.6) | copy-start | bytes 786436
  106.6 10.3 %copy-start = (bf16[512,256]{1,0:T(8,128)(2,1)}, bf16[512,256]{1,0:T(8,128)(2,1)S(1)}, u32[]{:S(2)}) copy-start(bf16[512,256]{1,0:T(8,128)(2,1)S(1)} %add_convert_fusion) | copy-start | bytes 786436
Sparse Core Ops, SparseCore 0:
  9.5 32.5 all-gather.3
  44.6 24.0 all-gather.5
  78.2 27.2 reduce-scatter.1
where the time goes:
time: 124 us; the launch traced here: 123 us
  waiting for transfers between devices  59.4 us (48%)
  blocking collectives  31.9 us (26%)
  between operations  13.8 us (11%)
  matrix products  8.6 us (7%)
  local copies, waits for them, and re-layouts  6 us (5%)
  other arithmetic  3.54 us (3%)
    reduce_scatter x1, waiting for transfers between devices, on_device(): lax.psum_scatter(partial_value.astype(jnp.bfloat16), 'mp', scatter_dimens...  27.4 us
    all_gather x1, waiting for transfers between devices, on_device(): lax.all_gather(input_weight, 'dp', axis=1, tiled=True)  25.1 us
    all_gather x1, blocking collectives, on_device(): lax.all_gather(pre_gain, 'mp', axis=0, tiled=True)  12.6 us
    all_gather x1, blocking collectives, on_device(): lax.all_gather(output_weight, 'dp', axis=1, tiled=True)  9.99 us
    psum x1, blocking collectives, on_device(): squares = lax.psum(jnp.sum(restored * restored, axis=1), 'mp')  9.28 us
    all_gather x1, waiting for transfers between devices, on_device(): lax.all_gather(tokens, 'mp', axis=1, tiled=True)  6.23 us
    unnamed x11, local copies, waits for them, and re-layouts  5.24 us
    dot_general x1, matrix products, one_sequence(): jnp.einsum('hqk,khd->qhd', probabilities, sequence_block[2], preferred_el...  2.86 us
  transfers between devices with their start and end apart: 3, of which 3 were waited for; matrix products, arithmetic and copies ran while one was open for 5% of the time, Pallas kernels for 0%

commit v1 on v0

--- a/solution.py
+++ b/solution.py
@@ -40,6 +40,34 @@
 
 
 def on_device(tokens, pre_gain, input_weight, output_weight, position_bias, post_gain):
+
+    def _begin_leaf(my_data):
+        passed = jax.lax.axis_index("dp")
+        state_next = jax.lax.axis_size("dp")
+        top, z1, s_next = (state_next, passed, my_data.shape[1])
+        field_out = jnp.zeros(
+            [dd * top if ix == 1 else dd for ix, dd in enumerate(my_data.shape)], my_data.dtype
+        )
+        d_next = lax.dynamic_update_slice_in_dim(field_out, my_data, z1 * s_next, axis=1)
+        t_next = b_now = my_data
+        for dev_j in range(1, top // 2 + 1):
+            before = range(top)
+            q_next = map(lambda ix: (ix, (ix + 1) % top), before)
+            outer = list(q_next)
+            t_next = jax.lax.ppermute(t_next, "dp", perm=outer)
+            d_next = lax.dynamic_update_slice_in_dim(
+                d_next, t_next, (z1 - dev_j) % top * s_next, axis=1
+            )
+            if 2 * dev_j < top:
+                formed = range(top)
+                y2 = map(lambda ix: (ix, (ix - 1) % top), formed)
+                side_arr = list(y2)
+                b_now = jax.lax.ppermute(b_now, "dp", side_arr)
+                d_next = lax.dynamic_update_slice_in_dim(
+                    d_next, b_now, (z1 + dev_j) % top * s_next, axis=1
+                )
+        return d_next
+
     rows_all, gain_all = (
         lax.all_gather(tokens, "mp", axis=1, tiled=True),
         lax.all_gather(pre_gain, "mp", axis=0, tiled=True),
@@ -49,10 +77,7 @@
     normed_in = (widened * inverse_rms * gain_all.astype(jnp.float32)).astype(jnp.bfloat16)
     feature_count = tokens.shape[1]
     projected = jnp.einsum(
-        "td,kdi->kti",
-        normed_in,
-        lax.all_gather(input_weight, "dp", axis=1, tiled=True),
-        preferred_element_type=jnp.float32,
+        "td,kdi->kti", normed_in, _begin_leaf(input_weight), preferred_element_type=jnp.float32
     )
     context = attend_all(projected.astype(jnp.bfloat16), position_bias)
     partial_value = jnp.dot(

time: 124 us -> 118 us (0.952)
  waiting for transfers between devices: 59.4 us -> 34.8 us
  local copies, waits for them, and re-layouts: 6 us -> 16.3 us
  starting transfers between devices: 0.12 us -> 9.1 us
    all_gather x1 -> x0, waiting for transfers between devices: 25.1 us -> none  [on_device(): lax.all_gather(input_weight, 'dp', axis=1, tiled=True)]
    ppermute x0 -> x7, waiting for transfers between devices: none -> 10.1 us  [the longest x4 9.31 us: _begin_leaf(): t_next = jax.lax.ppermute(t_next, 'dp', perm=outer)]
    ppermute x0 -> x7, starting transfers between devices: none -> 9.02 us  [the longest x3 7.9 us: _begin_leaf(): b_now = jax.lax.ppermute(b_now, 'dp', side_arr)]
    all_gather x1, waiting for transfers between devices: 6.23 us -> 0.01 us  [on_device(): lax.all_gather(tokens, 'mp', axis=1, tiled=True)]
    dynamic_update_slice x0 -> x8, local copies, waits for them, and re-layouts: none -> 5.71 us  [the longest x4 2.86 us: _begin_leaf(): lax.dynamic_update_slice_in_dim(d_next, t_next, (z1 - dev_j) % top * s_ne...]
    ppermute x0 -> x7, local copies, waits for them, and re-layouts: none -> 3.9 us  [the longest x4 2.49 us: _begin_leaf(): t_next = jax.lax.ppermute(t_next, 'dp', perm=outer)]
    reduce_scatter x1, waiting for transfers between devices: 27.4 us -> 23.9 us  [on_device(): lax.psum_scatter(partial_value.astype(jnp.bfloat16), 'mp', scatter_dimens...]
    broadcast_in_dim x0 -> x1, local copies, waits for them, and re-layouts: none -> 1.35 us  [_begin_leaf(): jnp.zeros([dd * top if ix == 1 else dd for ix, dd in enumerate(my_data.sh...]
  transfers between devices with their start and end apart: 3 -> 9, of which waited for: 3 -> 5; matrix products, arithmetic and copies ran while one was open for 5% -> 13% of each run, Pallas kernels for 0% -> 0%
where the time goes in v1:
time: 118 us
  waiting for transfers between devices  34.8 us (29%)
  blocking collectives  31.2 us (26%)
  local copies, waits for them, and re-layouts  16.3 us (14%)
  between operations  14.3 us (12%)
  starting transfers between devices  9.1 us (8%)
  matrix products  8.64 us (7%)
  other arithmetic  3.54 us (3%)
    reduce_scatter x1, waiting for transfers between devices, on_device(): lax.psum_scatter(partial_value.astype(jnp.bfloat16), 'mp', scatter_dimens...  23.9 us
    all_gather x1, blocking collectives, on_device(): lax.all_gather(pre_gain, 'mp', axis=0, tiled=True)  12 us
    all_gather x1, blocking collectives, on_device(): lax.all_gather(output_weight, 'dp', axis=1, tiled=True)  9.99 us
    ppermute x4, waiting for transfers between devices, _begin_leaf(): t_next = jax.lax.ppermute(t_next, 'dp', perm=outer)  9.31 us
    psum x1, blocking collectives, on_device(): squares = lax.psum(jnp.sum(restored * restored, axis=1), 'mp')  9.27 us
    ppermute x3, starting transfers between devices, _begin_leaf(): b_now = jax.lax.ppermute(b_now, 'dp', side_arr)  7.9 us
    unnamed x13, local copies, waits for them, and re-layouts  4.63 us
    dot_general x1, matrix products, one_sequence(): jnp.einsum('hqk,khd->qhd', probabilities, sequence_block[2], preferred_el...  2.93 us
  transfers between devices with their start and end apart: 9, of which 5 were waited for; matrix products, arithmetic and copies ran while one was open for 13% of the time, Pallas kernels for 0%

profile of v1, /device:TPU:0, one launch (start us, length us, event | category | flops | bytes accessed | tf_op | source)
XLA Modules:
  0.0 118.0 jit_solution(18387594913993419635)
XLA Ops:
  7.2 0.0 all-gather.3.cloned.1.call-start
  7.2 0.7 all-gather.3.cloned.1.call-update
  7.9 0.0 reduce-scatter.2.cloned.1.call-start
  7.9 0.5 collective-permute-start
  8.5 2.9 %collective-permute-start.1 = (bf16[3,128,256]{2,1,0:T(8,128)(2,1)}, bf16[3,128,256]{2,1,0:T(8,128)(2,1)S(1)}, u32[]{:S(2)}, u32[]{:S(2)}) collective-permute-start(bf16[3,128,256]{2,1,0:T(8,128)(2,1)} %param.8), channel_id=1, source_target_pairs={{0,28},{4,0},{8,4},{12,8},{16,12},{20,16},{24,20},{28,24},{1,29},{... | collective-permute-start | bytes 589832 | tf_op jit(solution)/shard_map/ppermute | solution.py:65
  11.4 1.1 copy.18
  12.7 0.7 reshape.34
  13.3 12.0 %all-gather = bf16[4,1,256]{2,1,0:T(2,128)(2,1)S(1)} all-gather(bf16[1,1,256]{2,1,0:T(2,128)(2,1)S(1)} %reshape.34), channel_id=1, replica_groups=mesh['dp'=8,'mp'=4] {'mp'}, dimensions={0}, use_global_device_ids=true | all-gather | bytes 2560 | tf_op jit(solution)/shard_map/all_gather | solution.py:73
  25.3 0.0 copy-start.3
  25.3 2.8 %copy.26 = bf16[4,512,512]{1,2,0:T(8,128)(2,1)S(1)} copy(bf16[4,512,512]{2,1,0:T(8,128)(2,1)} %param.10) | data formatting | bytes 4194304 | tf_op args[4]
  28.2 0.0 copy-done.3
  28.2 10.0 %all_gather.11 = bf16[256,1024]{1,0:T(8,128)(2,1)S(1)} all-gather(bf16[256,128]{1,0:T(8,128)(2,1)S(1)} %copy-done.3), channel_id=1, replica_groups=mesh['dp'=8,'mp'=4] {'dp'}, dimensions={1}, use_global_device_ids=true | all-gather | bytes 589824 | tf_op jit(solution)/shard_map/all_gather | solution.py:85
  38.2 1.3 %broadcast_in_dim.6 = bf16[3,1024,256]{1,2,0:T(8,128)(2,1)} broadcast(bf16[]{:T(256)} %constant.72.clone.1), dimensions={} | broadcast | bytes 1572866 | tf_op jit(solution)/shard_map/broadcast_in_dim | solution.py:48
  39.5 0.7 constant_dynamic-update-slice_fusion.7
  40.2 0.0 collective-permute-done
  40.2 0.2 copy.19
  40.4 0.5 collective-permute-start.2
  40.8 0.0 collective-permute-done.1
  40.8 0.2 copy.20
  41.0 2.3 %collective-permute-start.3 = (bf16[3,128,256]{2,1,0:T(8,128)(2,1)S(1)}, bf16[3,128,256]{2,1,0:T(8,128)(2,1)}, u32[]{:S(2)}, u32[]{:S(2)}) collective-permute-start(bf16[3,128,256]{2,1,0:T(8,128)(2,1)S(1)} %collective-permute-done.1), channel_id=1, source_target_pairs={{0,28},{4,0},{8,4},{12,8},{16,12},{20,16},{24,20},{28,24},{1,29},{... | collective-permute-start | bytes 589832 | tf_op jit(solution)/shard_map/ppermute | solution.py:65
  43.3 0.7 constant_dynamic-update-slice_fusion.6
  44.0 0.7 constant_dynamic-update-slice_fusion.5
  44.7 2.8 %collective-permute-done.2 = bf16[3,128,256]{2,1,0:T(8,128)(2,1)} collective-permute-done((bf16[3,128,256]{2,1,0:T(8,128)(2,1)S(1)}, bf16[3,128,256]{2,1,0:T(8,128)(2,1)}, u32[]{:S(2)}, u32[]{:S(2)}) %collective-permute-start.2) | collective-permute-done | bytes 196640 | tf_op jit(solution)/shard_map/ppermute | solution.py:57
  47.5 1.1 copy.21
  48.6 0.1 collective-permute-start.4
  48.7 0.0 collective-permute-done.3
  48.7 1.1 copy.22
  49.8 2.7 %collective-permute-start.5 = (bf16[3,128,256]{2,1,0:T(8,128)(2,1)}, bf16[3,128,256]{2,1,0:T(8,128)(2,1)S(1)}, u32[]{:S(2)}, u32[]{:S(2)}) collective-permute-start(bf16[3,128,256]{2,1,0:T(8,128)(2,1)} %collective-permute-done.3), channel_id=1, source_target_pairs={{0,28},{4,0},{8,4},{12,8},{16,12},{20,16},{24,20},{28,24},{1,29},{... | collective-permute-start | bytes 589832 | tf_op jit(solution)/shard_map/ppermute | solution.py:65
  52.4 0.7 constant_dynamic-update-slice_fusion.4
  53.2 0.7 constant_dynamic-update-slice_fusion.3
  53.9 2.9 %collective-permute-done.4 = bf16[3,128,256]{2,1,0:T(8,128)(2,1)S(1)} collective-permute-done((bf16[3,128,256]{2,1,0:T(8,128)(2,1)}, bf16[3,128,256]{2,1,0:T(8,128)(2,1)S(1)}, u32[]{:S(2)}, u32[]{:S(2)}) %collective-permute-start.4) | collective-permute-done | bytes 196640 | tf_op jit(solution)/shard_map/ppermute | solution.py:57
  56.7 0.2 copy.23
  56.9 0.1 collective-permute-start.6
  57.0 0.8 collective-permute-done.5
  57.8 0.2 copy.24
  57.9 0.7 constant_dynamic-update-slice_fusion.2
  58.7 0.7 constant_dynamic-update-slice_fusion.1
  59.4 3.6 %collective-permute-done.6 = bf16[3,128,256]{2,1,0:T(8,128)(2,1)} collective-permute-done((bf16[3,128,256]{2,1,0:T(8,128)(2,1)S(1)}, bf16[3,128,256]{2,1,0:T(8,128)(2,1)}, u32[]{:S(2)}, u32[]{:S(2)}) %collective-permute-start.6) | collective-permute-done | bytes 196640 | tf_op jit(solution)/shard_map/ppermute | solution.py:57
  63.0 1.1 copy.25
  64.1 0.7 constant_dynamic-update-slice_fusion
  64.9 0.0 all-gather.3.cloned.1.call-done
  64.9 1.5 %fusion.2 = f32[512]{0:T(512)S(1)} fusion(bf16[512,1024]{1,0:T(8,128)(2,1)} %all-gather.3.cloned.1.call-done), kind=kLoop, calls=%fused_computation.7 | loop fusion | flops 1572352 | bytes 1050624 | tf_op jit(solution)/shard_map/reduce_sum | solution.py:76
  66.4 2.8 %fusion.6 = bf16[3,512,256]{1,2,0:T(8,128)(2,1)S(1)} fusion(bf16[3,1024,256]{1,2,0:T(8,128)(2,1)} %constant_dynamic-update-slice_fusion, bf16[512,1024]{1,0:T(8,128)(2,1)} %all-gather.3.cloned.1.call-done, f32[1024]{0:T(1024)S(1)} %bitcast.26, f32[512]{0:T(512)S(1)} %add_rsqrt_fusion.1), kind=kOutput, calls=%fused_computation.13 | convolution fusion | flops 807796736 | bytes 3414016 | tf_op jit(solution)/shard_map/td,kdi->kti/dot_general | solution.py:79
  69.2 0.8 fusion.18
  69.9 0.0 copy-start.2
  69.9 1.5 %fusion.19 = f32[4,512]{1,0:T(4,128)S(1)} fusion(bf16[4,512,512]{1,2,0:T(8,128)(2,1)S(1)} %copy.26, bf16[512,4,64]{0,2,1:T(8,128)(2,1)S(1)} %bitcast.23, bf16[512,4,64]{0,2,1:T(8,128)(2,1)S(1)} %bitcast.21), kind=kOutput, calls=%fused_computation.37 | convolution fusion | flops 138412544 | bytes 2629632 | tf_op jit(solution)/shard_map/while/body/eval_jaxpr/sub | solution.py:31
  71.4 0.0 copy-done.2
  71.4 2.9 %fusion.7 = bf16[4,64,512]{2,1,0:T(8,128)(2,1)S(1)} fusion(bf16[512,4,64]{0,2,1:T(8,128)(2,1)} %bitcast.25, f32[4,512]{1,0:T(4,128)S(1)} %fusion.19, bf16[4,512,512]{1,2,0:T(8,128)(2,1)S(1)} %copy.26, bf16[512,4,64]{0,2,1:T(8,128)(2,1)} %bitcast.24, bf16[512,4,64]{0,2,1:T(8,128)(2,1)S(1)} %bitcast.22), kind=kOutput, calls=%fused_computation.14 | convolution fusion | flops 273811968 | bytes 3153920 | tf_op jit(solution)/shard_map/while/body/eval_jaxpr/hqk,khd->qhd/dot_general | solution.py:33
  74.3 0.0 copy-start.4
  74.4 0.0 copy-start.1
  74.4 1.4 %convolution_convert_fusion = bf16[512,1024]{1,0:T(8,128)(2,1)} fusion(bf16[512,256]{0,1:T(8,128)(2,1)S(1)} %bitcast.20, bf16[256,1024]{1,0:T(8,128)(2,1)S(1)} %all_gather.11), kind=kOutput, calls=%fused_computation.11 | convolution fusion | flops 268959744 | bytes 1835008 | tf_op jit(solution)/shard_map/dot_general | solution.py:83
  75.8 0.0 reduce-scatter.2.cloned.1.call-update
  75.8 0.0 copy-done.4
  75.9 23.9 %reduce-scatter.2.cloned.1.call-done = bf16[512,256]{1,0:T(8,128)(2,1)} async-done(((bf16[512,1024]{1,0:T(8,128)(2,1)}), bf16[512,256]{1,0:T(8,128)(2,1)}) %reduce-scatter.2.cloned.1.call-update) | async-done | bytes 262160 | tf_op jit(solution)/shard_map/reduce_scatter | solution.py:88
  99.8 0.0 copy-done.1
  99.8 1.0 add_convert_fusion
  100.8 0.0 copy-start
  100.8 0.1 fusion.12
  101.0 9.3 %psum.7 = f32[512]{0:T(512)S(1)} all-reduce(f32[512]{0:T(512)S(1)} %fusion.12), channel_id=1, replica_groups=mesh['dp'=8,'mp'=4] {'mp'}, use_global_device_ids=true, to_apply=%region_5.6 | all-reduce | flops 512 | bytes 4096 | tf_op jit(solution)/shard_map/psum | solution.py:93
  110.3 0.8 fusion.14
  111.1 0.0 copy-done
  (4 shorter events, 0.0 us)
Async XLA Ops:
  7.2 57.7 %all-gather.3.cloned.1.call-start = ((), (), s32[]{:S(2)}) async-start(), calls=%async_computation.1 | async-start | bytes 1310720 | tf_op jit(solution)/shard_map/all_gather | solution.py:72
  7.9 91.9 %reduce-scatter.2.cloned.1.call-start = ((), (), s32[]{:S(2)}) async-start(), calls=%async_computation.2 | async-start | bytes 1310720 | tf_op jit(solution)/shard_map/reduce_scatter | solution.py:88
  7.9 32.3 %collective-permute-start = (bf16[3,128,256]{2,1,0:T(8,128)(2,1)}, bf16[3,128,256]{2,1,0:T(8,128)(2,1)S(1)}, u32[]{:S(2)}, u32[]{:S(2)}) collective-permute-start(bf16[3,128,256]{2,1,0:T(8,128)(2,1)} %param.8), channel_id=1, source_target_pairs={{0,4},{4,8},{8,12},{12,16},{16,20},{20,24},{24,28},{28,0},{1,5},{5... | collective-permute-start | bytes 589832 | tf_op jit(solution)/shard_map/ppermute | solution.py:57
  8.5 32.3 %collective-permute-start.1 = (bf16[3,128,256]{2,1,0:T(8,128)(2,1)}, bf16[3,128,256]{2,1,0:T(8,128)(2,1)S(1)}, u32[]{:S(2)}, u32[]{:S(2)}) collective-permute-start(bf16[3,128,256]{2,1,0:T(8,128)(2,1)} %param.8), channel_id=1, source_target_pairs={{0,28},{4,0},{8,4},{12,8},{16,12},{20,16},{24,20},{28,24},{1,29},{... | collective-permute-start | bytes 589832 | tf_op jit(solution)/shard_map/ppermute | solution.py:65
  25.3 2.9 %copy-start.3 = (bf16[256,128]{1,0:T(8,128)(2,1)S(1)}, bf16[256,128]{1,0:T(8,128)(2,1)}, u32[]{:S(2)}) copy-start(bf16[256,128]{1,0:T(8,128)(2,1)} %param.9) | copy-start | bytes 196612
  40.4 7.1 %collective-permute-start.2 = (bf16[3,128,256]{2,1,0:T(8,128)(2,1)S(1)}, bf16[3,128,256]{2,1,0:T(8,128)(2,1)}, u32[]{:S(2)}, u32[]{:S(2)}) collective-permute-start(bf16[3,128,256]{2,1,0:T(8,128)(2,1)S(1)} %collective-permute-done), channel_id=1, source_target_pairs={{0,4},{4,8},{8,12},{12,16},{16,20},{20,24},{24,28},{28,0},{1,5},{5... | collective-permute-start | bytes 589832 | tf_op jit(solution)/shard_map/ppermute | solution.py:57
  41.0 7.7 %collective-permute-start.3 = (bf16[3,128,256]{2,1,0:T(8,128)(2,1)S(1)}, bf16[3,128,256]{2,1,0:T(8,128)(2,1)}, u32[]{:S(2)}, u32[]{:S(2)}) collective-permute-start(bf16[3,128,256]{2,1,0:T(8,128)(2,1)S(1)} %collective-permute-done.1), channel_id=1, source_target_pairs={{0,28},{4,0},{8,4},{12,8},{16,12},{20,16},{24,20},{28,24},{1,29},{... | collective-permute-start | bytes 589832 | tf_op jit(solution)/shard_map/ppermute | solution.py:65
  48.6 8.1 %collective-permute-start.4 = (bf16[3,128,256]{2,1,0:T(8,128)(2,1)}, bf16[3,128,256]{2,1,0:T(8,128)(2,1)S(1)}, u32[]{:S(2)}, u32[]{:S(2)}) collective-permute-start(bf16[3,128,256]{2,1,0:T(8,128)(2,1)} %collective-permute-done.2), channel_id=1, source_target_pairs={{0,4},{4,8},{8,12},{12,16},{16,20},{20,24},{24,28},{28,0},{1,5},{5... | collective-permute-start | bytes 589832 | tf_op jit(solution)/shard_map/ppermute | solution.py:57
  49.8 8.0 %collective-permute-start.5 = (bf16[3,128,256]{2,1,0:T(8,128)(2,1)}, bf16[3,128,256]{2,1,0:T(8,128)(2,1)S(1)}, u32[]{:S(2)}, u32[]{:S(2)}) collective-permute-start(bf16[3,128,256]{2,1,0:T(8,128)(2,1)} %collective-permute-done.3), channel_id=1, source_target_pairs={{0,28},{4,0},{8,4},{12,8},{16,12},{20,16},{24,20},{28,24},{1,29},{... | collective-permute-start | bytes 589832 | tf_op jit(solution)/shard_map/ppermute | solution.py:65
  56.9 6.2 %collective-permute-start.6 = (bf16[3,128,256]{2,1,0:T(8,128)(2,1)S(1)}, bf16[3,128,256]{2,1,0:T(8,128)(2,1)}, u32[]{:S(2)}, u32[]{:S(2)}) collective-permute-start(bf16[3,128,256]{2,1,0:T(8,128)(2,1)S(1)} %collective-permute-done.4), channel_id=1, source_target_pairs={{0,4},{4,8},{8,12},{12,16},{16,20},{20,24},{24,28},{28,0},{1,5},{5... | collective-permute-start | bytes 589832 | tf_op jit(solution)/shard_map/ppermute | solution.py:57
  69.9 1.5 %copy-start.2 = (bf16[1,512,256]{1,2,0:T(8,128)(2,1)}, bf16[1,512,256]{1,2,0:T(8,128)(2,1)S(1)}, u32[]{:S(2)}) copy-start(bf16[1,512,256]{1,2,0:T(8,128)(2,1)S(1)} %get-tuple-element.11) | copy-start | bytes 786436
  74.3 1.5 %copy-start.4 = (bf16[256]{0:T(256)(128)(2,1)S(1)}, bf16[256]{0:T(256)(128)(2,1)}, u32[]{:S(2)}) copy-start(bf16[256]{0:T(256)(128)(2,1)} %param.11) | copy-start | bytes 1540
  74.4 25.5 %copy-start.1 = (bf16[512,256]{1,0:T(8,128)(2,1)S(1)}, bf16[512,256]{1,0:T(8,128)(2,1)}, u32[]{:S(2)}) copy-start(bf16[512,256]{1,0:T(8,128)(2,1)} %param.6) | copy-start | bytes 786436
  100.8 10.3 %copy-start = (bf16[512,256]{1,0:T(8,128)(2,1)}, bf16[512,256]{1,0:T(8,128)(2,1)S(1)}, u32[]{:S(2)}) copy-start(bf16[512,256]{1,0:T(8,128)(2,1)S(1)} %add_convert_fusion) | copy-start | bytes 786436
Sparse Core Ops, SparseCore 0:
  9.5 32.6 all-gather.2
  76.0 23.8 reduce-scatter.1
